TPU v7x, 32 devices: a whole 2x2x4 slice. The times are simulated.
32 devices in a mesh: dp: 8 (over y, x, core), tensor: 4 (over z).
Axes of the slice: x: 2, y: 2, z: 4, core: 2. Of those that a mesh axis runs over, the one named last changes fastest.
Arguments:
- rollout: bfloat16 [2048, 6144], P('dp', 'tensor'), may hold values from -100 to 100
- lengths: int32 [8, 32], replicated, may hold values from 1 to 8, as said below
- packing: int32 [256], replicated, may hold values from 0 to 255, as said below
- norm_gain: float32 [6144], replicated, may hold values from 0.5 to 4
- query_weight: bfloat16 [6144, 1024], P(None, 'tensor'), may hold values from -0.078125 to 0.078125
- keyval_weight: bfloat16 [6144, 256], P(None, 'tensor'), may hold values from -0.078125 to 0.078125
- out_weight: bfloat16 [1024, 6144], P('tensor'), may hold values from -0.1875 to 0.1875
Outputs:
- layer_out: bfloat16 [2048, 6144], P('dp', 'tensor')
Inputs may be any that keep to these rules, and one draw needn't show every extreme that they name: lengths[s, k] is the number of tokens of response k of source s; some response has 8 tokens in every draw. `packing`: a permutation of 0 .. 255; response r comes from source r // 32; every owner receives exactly 32 responses, exactly 4 of them from each source.
All inputs are finite; a program needn't handle non-finite values.
Results may differ from a plain program's by a relative error of at most 0.015.
Values may be sent and summed in bfloat16 or wider, within the bound.
A program may use at most 64 MiB of HBM per device.

v0:
```python
import math

import jax
import jax.numpy as jnp
from jax import lax
from jax.sharding import PartitionSpec as P

D = 6144
HD = 128
HQ_DEV = 2
GROUP = 8


epsilon = 1e-05
rope_base = 500000.0


def owner_map(lengths, packing, owner_id, pack_len):
    per_source = lengths.shape[1]
    chosen = lax.dynamic_slice_in_dim(packing, owner_id * per_source, per_source)
    ordered = jnp.take(lengths.reshape(-1), chosen)
    doc_start = jnp.cumsum(ordered) - ordered
    places = jnp.arange(pack_len, dtype=jnp.int32)
    inside = (places[:, None] >= doc_start[None, :]) & (
        places[:, None] < (doc_start + ordered)[None, :]
    )
    is_valid = jnp.any(inside, axis=1)
    slot_of = jnp.sum(
        jnp.where(inside, jnp.arange(per_source, dtype=jnp.int32)[None, :], 0), axis=1
    )
    response = jnp.take(chosen, slot_of)
    position = jnp.where(is_valid, places - jnp.take(doc_start, slot_of), 0)
    doc_id = jnp.where(is_valid, slot_of, per_source)
    return (response, position, doc_id, is_valid)


def rotate(values, position, head_dim):
    half_dim = head_dim // 2
    frequency = rope_base ** (-jnp.arange(half_dim, dtype=jnp.float32) * 2.0 / head_dim)
    angles = position.astype(jnp.float32)[:, None] * frequency[None, :]
    cosine = jnp.concatenate([jnp.cos(angles), jnp.cos(angles)], axis=1)[:, None, :]
    sine_table = jnp.concatenate([jnp.sin(angles), jnp.sin(angles)], axis=1)[:, None, :]
    turned = jnp.concatenate([-values[..., half_dim:], values[..., :half_dim]], axis=-1)
    return values * cosine + turned * sine_table


def body(rollout, lengths, packing, norm_gain, query_weight, keyval_weight, out_weight):
    owner_id = lax.axis_index("dp")
    tensor_index = lax.axis_index("tensor")
    tensor_count = lax.axis_size("tensor")
    pack_len = rollout.shape[0]
    per_source = lengths.shape[1]
    response, position, doc_id, is_valid = owner_map(lengths, packing, owner_id, pack_len)
    source_start = jnp.cumsum(lengths, axis=1) - lengths
    global_row = (
        response // per_source * pack_len + jnp.take(source_start.reshape(-1), response) + position
    )
    portion = lax.all_gather(rollout, "dp", axis=0, tiled=True)
    within = is_valid & (global_row >= 0) & (global_row < portion.shape[0])
    picked = jnp.take(portion, jnp.clip(global_row, 0, portion.shape[0] - 1), axis=0)
    packed = jnp.where(within[:, None], picked, jnp.zeros_like(rollout))
    widened = lax.all_gather(packed, "tensor", axis=1, tiled=True).astype(jnp.float32)
    scaled = (widened * norm_gain[None, :]).astype(jnp.bfloat16)
    query_acc = jnp.dot(scaled, query_weight, preferred_element_type=jnp.float32)
    keyval_acc = jnp.dot(scaled, keyval_weight, preferred_element_type=jnp.float32)
    squares = jnp.sum(widened * widened, axis=1)
    query_acc, keyval_acc, squares = (query_acc, keyval_acc, squares)
    inverse = lax.rsqrt(squares / D + epsilon)
    queries = query_acc * inverse[:, None]
    keyval_share = (keyval_acc * inverse[:, None]).astype(jnp.bfloat16)
    keyval_all = lax.all_gather(keyval_share, "tensor", axis=1, tiled=True)
    kv_count = keyval_weight.shape[1] * tensor_count // (2 * HD)
    shared_head = tensor_index * HQ_DEV // GROUP
    keys = lax.dynamic_slice_in_dim(keyval_all, shared_head * HD, HD, 1)
    values = lax.dynamic_slice_in_dim(keyval_all, (kv_count + shared_head) * HD, HD, 1)
    q_rot = rotate(queries.reshape(pack_len, HQ_DEV, HD), position, HD).astype(jnp.bfloat16)
    k_rot = rotate(keys.astype(jnp.float32)[:, None, :], position, HD)[:, 0, :].astype(jnp.bfloat16)
    scores = jnp.einsum(
        "qhd,kd->hqk", q_rot, k_rot, preferred_element_type=jnp.float32
    ) / math.sqrt(HD)
    places = jnp.arange(pack_len, dtype=jnp.int32)
    allowed = (doc_id[:, None] == doc_id[None, :]) & (places[None, :] <= places[:, None])
    masked = jnp.where(allowed[None], scores, -jnp.inf)
    row_max = jnp.max(masked, axis=2, keepdims=True)
    exponent = jnp.exp(masked - row_max)
    weights = (exponent / jnp.sum(exponent, axis=2, keepdims=True)).astype(jnp.bfloat16)
    context = jnp.einsum("hqk,kd->qhd", weights, values, preferred_element_type=jnp.float32)
    context = context.astype(jnp.bfloat16).reshape(pack_len, HQ_DEV * HD)
    partial_sum = jnp.dot(context, out_weight, preferred_element_type=jnp.float32)
    summed = lax.psum_scatter(
        partial_sum.astype(jnp.bfloat16), "tensor", scatter_dimension=1, tiled=True
    ).astype(jnp.float32)
    result = jnp.where(is_valid[:, None], summed + packed.astype(jnp.float32), 0.0)
    return result.astype(jnp.bfloat16)


def solution(mesh):
    in_specs = (
        P("dp", "tensor"),
        P(),
        P(),
        P(),
        P(None, "tensor"),
        P(None, "tensor"),
        P("tensor", None),
    )
    out_specs = P("dp", "tensor")
    return jax.shard_map(body, mesh=mesh, in_specs=in_specs, out_specs=out_specs, check_vma=False)
```

profile of v0, /device:TPU:0, one launch (start us, length us, event | category | flops | bytes accessed | tf_op | source)
XLA Modules:
  0.0 227.3 jit_solution(16946760604739307667)
XLA Ops:
  6.5 0.7 all-gather.3.cloned.1.call-update
  7.3 0.9 reshape.142
  8.2 0.9 reduce_window_sum.18
  9.1 0.8 compare_select_fusion.2
  9.9 0.7 gather_fusion
  10.7 0.1 reduce
  10.9 0.7 sub.31
  11.6 0.7 fusion.52
  12.3 0.7 fusion.51
  13.1 0.1 select_reduce_fusion
  13.2 20.2 %add_select_fusion = (s32[256]{0:T(256)S(1)}, s32[256]{0:T(256)S(1)}) fusion(s32[]{:T(128)} %bitcast.32, s32[]{:T(128)} %bitcast.31, s32[]{:T(128)} %bitcast.30, s32[]{:T(128)} %bitcast.29, s32[]{:T(128)} %bitcast.28, s32[]{:T(128)} %bitcast.27, s32[]{:T(128)} %bitcast.26, s32[]{:T(128)} %bitcast.25, s32[]{:T(128)} %bitcast.24, s32[]{:T(128)} %bitcast.23, ...), kind=kLoop, calls=%fused_computation.63 | loop fusion | flops 18432 | bytes 3200 | tf_op jit(solution)/shard_map/jit(_take)/jit(_where)/select_n | solution.py:56
  33.4 1.9 gather_fusion.1
  35.3 0.7 fusion.54
  36.0 0.7 fusion.53
  36.8 0.1 fusion.31
  36.9 20.2 %fusion.48 = (f32[256]{0:T(256)S(1)}, s32[256]{0:T(256)S(1)}) fusion(pred[256]{0:T(512)(128)(4,1)S(1)} %fusion.31, s32[]{:T(128)} %bitcast.64, s32[]{:T(128)} %bitcast.63, s32[]{:T(128)} %bitcast.62, s32[]{:T(128)} %bitcast.61, s32[]{:T(128)} %bitcast.60, s32[]{:T(128)} %bitcast.59, s32[]{:T(128)} %bitcast.58, s32[]{:T(128)} %bitcast.57, s32[]{:T(128)} %bitcast.56, ...), kind=kLoop, calls=%fused_computation.115 | loop fusion | flops 18432 | bytes 3456 | tf_op jit(solution)/shard_map/convert_element_type | solution.py:40
  57.1 0.3 all-gather.3.cloned.1.call-done
  57.4 6.5 %gather_fusion.2 = bf16[256,1536]{1,0:T(8,128)(2,1)} fusion(bf16[2048,1536]{1,0:T(8,128)(2,1)} %all-gather.3.cloned.1.call-done, s32[1024]{0:T(1024)S(1)} %pad_clamp_fusion), kind=kCustom, calls=%fused_computation.2 | custom fusion | bytes 1573888 | tf_op jit(solution)/shard_map/jit(_take)/gather | solution.py:60
  63.9 2.2 select_select_fusion
  66.2 0.3 multiply_cosine_fusion
  66.5 0.7 fusion.21
  67.2 64.9 %all-gather.5.cloned.1.call-done = bf16[256,6144]{1,0:T(8,128)(2,1)} async-done(((bf16[256,1536]{1,0:T(8,128)(2,1)}), bf16[256,6144]{1,0:T(8,128)(2,1)}) %all-gather.5.cloned.1.call-update) | async-done | bytes 3145744 | tf_op jit(solution)/shard_map/all_gather | solution.py:62
  132.1 2.7 %fusion.2 = f32[256]{0:T(256)S(1)} fusion(bf16[256,6144]{1,0:T(8,128)(2,1)} %all-gather.5.cloned.1.call-done), kind=kLoop, calls=%fused_computation.8 | loop fusion | flops 4718336 | bytes 3146752 | tf_op jit(solution)/shard_map/reduce_sum | solution.py:66
  135.0 2.4 %fusion.17 = bf16[256,64]{0,1:T(8,128)(2,1)S(1)} fusion(bf16[6144,64]{0,1:T(8,128)(2,1)} %param.14, bf16[256,6144]{1,0:T(8,128)(2,1)S(1)} %copy-done.1, f32[6144]{0:T(1024)} %param.12, f32[256]{0:T(256)S(1)} %add_rsqrt_fusion), kind=kOutput, calls=%fused_computation.20 | convolution fusion | flops 206077952 | bytes 3990528 | tf_op jit(solution)/shard_map/dot_general | solution.py:65
  137.3 13.4 %all_gather.11 = bf16[256,256]{0,1:T(8,128)(2,1)S(1)} all-gather(bf16[256,64]{0,1:T(8,128)(2,1)S(1)} %fusion.17), channel_id=1, replica_groups=mesh['dp'=8,'tensor'=4] {'tensor'}, dimensions={1}, use_global_device_ids=true | all-gather | bytes 163840 | tf_op jit(solution)/shard_map/all_gather | solution.py:71
  150.8 1.4 fusion.11
  152.4 1.0 fusion.10
  153.5 1.3 fusion.55
  154.8 1.5 convolution_convert_fusion.1
  156.3 2.7 %convolution_convert_fusion = bf16[256,6144]{1,0:T(8,128)(2,1)} fusion(bf16[256,256]{0,1:T(8,128)(2,1)S(1)} %bitcast.113, bf16[256,6144]{1,0:T(8,128)(2,1)S(1)} %copy-done), kind=kOutput, calls=%fused_computation.6 | convolution fusion | flops 806879232 | bytes 6422528 | tf_op jit(solution)/shard_map/dot_general | solution.py:89
  159.0 59.1 %reduce-scatter.2.cloned.1.call-done = bf16[256,1536]{1,0:T(8,128)(2,1)} async-done(((bf16[256,6144]{1,0:T(8,128)(2,1)}), bf16[256,1536]{1,0:T(8,128)(2,1)}) %reduce-scatter.2.cloned.1.call-update) | async-done | bytes 786448 | tf_op jit(solution)/shard_map/reduce_scatter | solution.py:90
  218.1 2.7 %select_convert_fusion = bf16[256,1536]{1,0:T(8,128)(2,1)} fusion(bf16[256,1536]{1,0:T(8,128)(2,1)} %reduce-scatter.2.cloned.1.call-done, pred[256]{0:T(512)(128)(4,1)S(1)} %fusion.31, bf16[256,1536]{1,0:T(8,128)(2,1)} %gather_fusion.2, pred[256]{0:T(512)(128)(4,1)S(1)} %copy-done.7, pred[256]{0:T(512)(128)(4,1)S(1)} %get-tuple-element.8), kind=kLoop, calls=%fused_computation.11 | loop fusion | flops 2752512 | bytes 2360064 | tf_op jit(solution)/shard_map/convert_element_type | solution.py:94
  (45 shorter events, 0.7 us)
Async XLA Ops:
  6.5 149.8 %copy-start = (bf16[256,6144]{1,0:T(8,128)(2,1)S(1)}, bf16[256,6144]{1,0:T(8,128)(2,1)}, u32[]{:S(2)}) copy-start(bf16[256,6144]{1,0:T(8,128)(2,1)} %param.15) | copy-start | bytes 9437188
  6.5 50.9 %all-gather.3.cloned.1.call-start = ((), (), s32[]{:S(2)}) async-start(), calls=%async_computation.1 | async-start | bytes 7077888 | tf_op jit(solution)/shard_map/all_gather | solution.py:58
  7.3 124.9 %all-gather.5.cloned.1.call-start = ((), (), s32[]{:S(2)}) async-start(), calls=%async_computation.2 | async-start | bytes 3932160 | tf_op jit(solution)/shard_map/all_gather | solution.py:62
  57.1 6.8 %copy-start.6 = (pred[256]{0:T(512)(128)(4,1)}, pred[256]{0:T(512)(128)(4,1)S(1)}, u32[]{:S(2)}) copy-start(pred[256]{0:T(512)(128)(4,1)S(1)} %compare_and_fusion.1) | copy-start | bytes 772
  66.1 152.0 %reduce-scatter.2.cloned.1.call-start = ((), (), s32[]{:S(2)}) async-start(), calls=%async_computation.3 | async-start | bytes 3932160 | tf_op jit(solution)/shard_map/reduce_scatter | solution.py:90
  132.1 2.8 %copy-start.1 = (bf16[256,6144]{1,0:T(8,128)(2,1)S(1)}, bf16[256,6144]{1,0:T(8,128)(2,1)}, u32[]{:S(2)}) copy-start(bf16[256,6144]{1,0:T(8,128)(2,1)} %all-gather.5.cloned.1.call-done) | copy-start | bytes 9437188
  134.9 15.9 %copy-start.8 = (bf16[6144,256]{1,0:T(8,128)(2,1)S(1)}, bf16[6144,256]{1,0:T(8,128)(2,1)}, u32[]{:S(2)}) copy-start(bf16[6144,256]{1,0:T(8,128)(2,1)} %param.13) | copy-start | bytes 9437188
  134.9 15.9 %copy-start.9 = (f32[6144]{0:T(1024)S(1)}, f32[6144]{0:T(1024)}, u32[]{:S(2)}) copy-start(f32[6144]{0:T(1024)} %param.12) | copy-start | bytes 73732
  150.7 1.6 copy-start.2
  150.8 1.6 copy-start.4
  150.8 1.6 copy-start.5
  150.8 1.6 copy-start.3
  159.0 59.1 %copy-start.7 = (pred[256]{0:T(512)(128)(4,1)S(1)}, pred[256]{0:T(512)(128)(4,1)}, u32[]{:S(2)}) copy-start(pred[256]{0:T(512)(128)(4,1)} %copy-done.6) | copy-start | bytes 772
Sparse Core Ops, SparseCore 0:
  9.2 48.1 all-gather.2
  66.2 65.8 all-gather.4
  159.1 58.9 reduce-scatter.1
where the time goes:
time: 228 us; the launch traced here: 227 us
  waiting for transfers between devices  125 us (55%)
  other arithmetic  51.9 us (23%)
  blocking collectives  13.4 us (6%)
  between operations  13.4 us (6%)
  local copies, waits for them, and re-layouts  13.2 us (6%)
  matrix products  10.3 us (5%)
    all_gather x1, waiting for transfers between devices, body(): lax.all_gather(packed, 'tensor', axis=1, tiled=True).astype(jnp.float32)  64.9 us
    reduce_scatter x1, waiting for transfers between devices, body(): lax.psum_scatter(partial_sum.astype(jnp.bfloat16), 'tensor', scatter_dime...  59.1 us
    select_n x1, other arithmetic, body(): jnp.take(source_start.reshape(-1), response)  20.2 us
    convert_element_type x1, other arithmetic, rotate(): angles = position.astype(jnp.float32)[:, None] * frequency[None, :]  20.2 us
    all_gather x1, blocking collectives, body(): keyval_all = lax.all_gather(keyval_share, 'tensor', axis=1, tiled=True)  13.4 us
    gather x1, local copies, waits for them, and re-layouts, body(): jnp.take(portion, jnp.clip(global_row, 0, portion.shape[0] - 1), axis=0)  6.47 us
  transfers between devices with their start and end apart: 3, of which 3 were waited for; matrix products, arithmetic and copies ran while one was open for 22% of the time, Pallas kernels for 0%

commit v1 on v0

--- a/solution.py
+++ b/solution.py
@@ -1,8 +1,12 @@
+import functools
 import math
 
+import numpy as np
 import jax
 import jax.numpy as jnp
 from jax import lax
+from jax.experimental import pallas as pl
+from jax.experimental.pallas import tpu as pltpu
 from jax.sharding import PartitionSpec as P
 
 D = 6144
@@ -44,7 +48,7 @@
     return values * cosine + turned * sine_table
 
 
-def body(rollout, lengths, packing, norm_gain, query_weight, keyval_weight, out_weight):
+def plain_body(rollout, lengths, packing, norm_gain, query_weight, keyval_weight, out_weight):
     owner_id = lax.axis_index("dp")
     tensor_index = lax.axis_index("tensor")
     tensor_count = lax.axis_size("tensor")
@@ -94,6 +98,381 @@
     return result.astype(jnp.bfloat16)
 
 
+MESH = pl.DeviceIdType.MESH
+CORES = 2
+HALO = 16
+
+
+def aligned(index, size):
+    return pl.multiple_of(index * size, size)
+
+
+def fused_kernel(
+    cfg, pk_col, pk_row, len_col, len_row, gain, cos_tab, sin_tab, roll_in, w_in, o_in, out,
+    wbuf, obuf, sendb, recvb, packed, scaled, q_part, kv_part, kv_acc, q_recv, kv_recv, ctx,
+    pos_buf, valid_buf, send_sems, recv_sems, local_sems,
+):
+    n_dp, n_t, length, feat, per_source = cfg
+    chips = n_dp // CORES
+    w_sub = wbuf.shape[1] // n_dp
+    o_rows = o_in.shape[0]
+    o_sub = o_rows // n_dp
+    block = length // n_dp
+    most = length // per_source
+    rows = length // n_t
+    qd = w_in.shape[2]
+    quarter = feat // 4
+    me = lax.axis_index("dp")
+    t = lax.axis_index("tensor")
+    core = lax.rem(me, CORES)
+    chip = lax.div(me, CORES)
+    partner = chip * CORES + (CORES - 1 - core)
+
+    def t_at(k):
+        return lax.rem(t + k, n_t)
+
+    def chip_at(k):
+        return lax.rem(chip + k, chips) * CORES + core
+
+    barrier = pltpu.get_barrier_semaphore()
+    for k in range(1, n_dp):
+        pl.semaphore_signal(
+            barrier, inc=1, device_id=(lax.rem(me + k, n_dp), t), device_id_type=MESH
+        )
+    for k in range(1, n_t):
+        pl.semaphore_signal(barrier, inc=1, device_id=(me, t_at(k)), device_id_type=MESH)
+    pl.semaphore_wait(barrier, n_dp + n_t - 2)
+
+    started = []
+
+    def send(source, target, device):
+        at = len(started)
+        copy = pltpu.make_async_remote_copy(
+            src_ref=source,
+            dst_ref=target,
+            send_sem=send_sems.at[at],
+            recv_sem=recv_sems.at[at],
+            device_id=device,
+            device_id_type=MESH,
+        )
+        copy.start()
+        started.append(copy)
+        return copy
+
+    w_first, o_first = {}, {}
+    for k in range(1, n_t):
+        to = t_at(k)
+        w_first[k] = send(
+            w_in.at[to, pl.ds(aligned(me, w_sub), w_sub)],
+            wbuf.at[t, pl.ds(aligned(me, w_sub), w_sub)],
+            (me, to),
+        )
+    own_w = pltpu.make_async_copy(w_in.at[t], wbuf.at[t], local_sems.at[0])
+    own_w.start()
+    for k in range(1, n_t):
+        to = t_at(k)
+        o_first[k] = send(
+            o_in.at[pl.ds(aligned(me, o_sub), o_sub), pl.ds(aligned(to, feat), feat)],
+            obuf.at[t, pl.ds(aligned(me, o_sub), o_sub)],
+            (me, to),
+        )
+    own_o = pltpu.make_async_copy(
+        o_in.at[:, pl.ds(aligned(t, feat), feat)], obuf.at[t], local_sems.at[1]
+    )
+    own_o.start()
+
+    down = lax.broadcasted_iota(jnp.int32, (length, length), 0).astype(jnp.float32)
+    across = lax.broadcasted_iota(jnp.int32, (length, length), 1).astype(jnp.float32)
+
+    def part(value, size):
+        return jnp.floor((value + 0.5) * (1.0 / size))
+
+    def pick(mask, value, axis):
+        return jnp.sum(jnp.where(mask, value, 0.0), axis=axis, keepdims=True)
+
+    same = part(down, per_source) == part(across, per_source)
+    len_c, len_r = len_col[...], len_row[...]
+    pk_c, pk_r = pk_col[...], pk_row[...]
+    src_start = pick(same & (across < down), len_r, 1)
+    chosen = down == pk_r
+    q_len_r = pick(chosen, len_c, 0)
+    q_start_r = pick(chosen, src_start, 0)
+    q_len_c = pick(across == pk_c, len_r, 1)
+    earlier = same & (down < across)
+    doc_start_r = pick(earlier, q_len_c, 0)
+    q_src_r = part(pk_r, per_source)
+    slot_r = pick(earlier & (part(pk_c, per_source) == q_src_r), 1.0, 0)
+    mine = me.astype(jnp.float32)
+    across_1 = across[:1]
+    down_1 = down[:, :1]
+    owner_r = part(across_1, per_source)
+    target = jnp.where(q_src_r == mine, owner_r * (per_source // n_dp) + slot_r, -1.0)
+    group = part(down_1, most)
+    match = target == group
+    token = down_1 - group * most
+    row_sent = jnp.where(token < pick(match, q_len_r, 1), pick(match, q_start_r, 1) + token, -1.0)
+    take_send = (across == row_sent).astype(jnp.float32).astype(jnp.bfloat16)
+    inside = (owner_r == mine) & (doc_start_r <= down) & (down < doc_start_r + q_len_r)
+    is_valid = pick(inside, 1.0, 1)
+    position = (down_1 - pick(inside, doc_start_r, 1)) * is_valid
+    row_got = jnp.where(
+        is_valid > 0.0, pick(inside, q_src_r * block + slot_r * most, 1) + position, -1.0
+    )
+    take_recv = (across == row_got).astype(jnp.float32).astype(jnp.bfloat16)
+    pos_buf[:HALO, :] = jnp.zeros((HALO, HD), jnp.float32)
+    pos_buf[HALO:, :] = jnp.broadcast_to(position, (length, HD))
+    valid_buf[...] = jnp.broadcast_to(is_valid, (length, HD))
+
+    tile = 256
+    tiles = feat // tile
+
+    def send_tile(i, carry):
+        at = pl.ds(aligned(i, tile), tile)
+        sendb[:, at] = jnp.dot(
+            take_send, roll_in[:, at], preferred_element_type=jnp.float32
+        ).astype(jnp.bfloat16)
+        return carry
+
+    lax.fori_loop(0, tiles, send_tile, 0)
+
+    rows_of = {}
+    for k in range(1, n_dp):
+        to = lax.rem(me + k, n_dp)
+        rows_of[k] = send(
+            sendb.at[pl.ds(aligned(to, block), block)],
+            recvb.at[pl.ds(aligned(me, block), block)],
+            (to, t),
+        )
+    keep = pl.ds(aligned(me, block), block)
+    recvb[keep, :] = sendb[keep, :]
+
+    def spread(buf, first, sub):
+        hops = {}
+        for j in range(1, n_t):
+            first[j].wait_recv()
+            at = buf.at[t_at(n_t - j), pl.ds(aligned(me, sub), sub)]
+            for k in range(1, chips):
+                hops[j, k] = send(at, at, (chip_at(k), t))
+        return hops
+
+    def share(buf, hops, sub):
+        last = []
+        for k in range(chips):
+            for j in range(1, n_t):
+                if k:
+                    hops[j, k].wait_recv()
+                at = buf.at[
+                    t_at(n_t - j), pl.ds(aligned(chip_at(chips - k if k else 0), sub), sub)
+                ]
+                last.append(send(at, at, (partner, t)))
+        return last
+
+    w_hops = spread(wbuf, w_first, w_sub)
+
+    for k in range(1, n_dp):
+        rows_of[k].wait_recv()
+
+    def pack_tile(i, total):
+        at = pl.ds(aligned(i, tile), tile)
+        x = jnp.dot(take_recv, recvb[:, at], preferred_element_type=jnp.float32)
+        packed[:, at] = x.astype(jnp.bfloat16)
+        g = gain[:, pl.ds(pl.multiple_of(t * feat + i * tile, tile), tile)]
+        scaled[:, at] = (x * g).astype(jnp.bfloat16)
+        return total + jnp.sum(x * x, axis=1, keepdims=True)
+
+    squares = lax.fori_loop(0, tiles, pack_tile, jnp.zeros((length, 1), jnp.float32))
+    lane = lax.broadcasted_iota(jnp.int32, (length, HD), 1)
+    high = squares.astype(jnp.bfloat16).astype(jnp.float32)
+    kv_part[:HALO, :] = jnp.zeros((HALO, 3 * HD), jnp.bfloat16)
+    kv_part[HALO:, 2 * HD :] = jnp.where(
+        lane < HD // 2, jnp.broadcast_to(high, (length, HD)), jnp.broadcast_to(squares - high, (length, HD))
+    ).astype(jnp.bfloat16)
+
+    o_hops = spread(obuf, o_first, o_sub)
+    w_last = share(wbuf, w_hops, w_sub)
+    own_w.wait()
+    for copy in w_last:
+        copy.wait_recv()
+
+    def project(u, carry):
+        x = scaled[...]
+        q_part[:, pl.ds(aligned(u, qd), qd)] = jnp.dot(
+            x, wbuf[u, :feat, :], preferred_element_type=jnp.float32
+        ).astype(jnp.bfloat16)
+        w = wbuf[u, feat:, :]
+        y = jnp.dot(x[:, :quarter], w, preferred_element_type=jnp.float32)
+        for i in range(1, 4):
+            z = jnp.dot(
+                x[:, i * quarter : (i + 1) * quarter], w, preferred_element_type=jnp.float32
+            )
+            y += pltpu.roll(z, qd - i * (qd // 4), 1)
+        kv_acc[u] = y[:, :HD]
+        return carry
+
+    lax.fori_loop(0, n_t, project, 0)
+    for i in range(2):
+        kv_part[HALO:, i * HD : (i + 1) * HD] = jnp.where(
+            lane < HD // 2, kv_acc[2 * i], pltpu.roll(kv_acc[2 * i + 1], HD // 2, 1)
+        ).astype(jnp.bfloat16)
+
+    shares = []
+    for k in range(1, n_t):
+        to = t_at(k)
+        shares.append(
+            send(
+                kv_part.at[pl.ds(aligned(to, rows), rows + HALO)], kv_recv.at[k - 1], (me, to)
+            )
+        )
+        shares.append(
+            send(q_part.at[pl.ds(aligned(to, rows), rows)], q_recv.at[k - 1], (me, to))
+        )
+    o_last = share(obuf, o_hops, o_sub)
+
+    for copy in shares:
+        copy.wait_recv()
+    keys_at = pl.ds(aligned(t, rows), rows + HALO)
+    queries_at = pl.ds(aligned(t, rows), rows)
+    kv = kv_part[keys_at, :].astype(jnp.float32)
+    for k in range(n_t - 1):
+        kv += kv_recv[k].astype(jnp.float32)
+    sums = jnp.sum(kv[:, 2 * HD :], axis=1, keepdims=True) * (2.0 / HD)
+    inverse = lax.rsqrt(sums / (feat * n_t) + epsilon)
+    kv_bf = (kv[:, : 2 * HD] * inverse).astype(jnp.bfloat16)
+    values = kv_bf[:, HD:]
+    pos = pos_buf[keys_at, :]
+    cosine = jnp.zeros((rows + HALO, HD), jnp.float32)
+    sine = jnp.zeros((rows + HALO, HD), jnp.float32)
+    for m in range(most):
+        at_m = pos == float(m)
+        cosine = jnp.where(at_m, cos_tab[m : m + 1, :], cosine)
+        sine = jnp.where(at_m, sin_tab[m : m + 1, :], sine)
+
+    def turn(v, c, s):
+        return v * c + pltpu.roll(v, HD // 2, 1) * s
+
+    k_rot = turn(kv_bf[:, :HD].astype(jnp.float32), cosine, sine).astype(jnp.bfloat16)
+    q_down = lax.broadcasted_iota(jnp.int32, (rows, rows + HALO), 0).astype(jnp.float32)
+    k_across = lax.broadcasted_iota(jnp.int32, (rows, rows + HALO), 1).astype(jnp.float32) - HALO
+    allowed = (k_across <= q_down) & (k_across >= q_down - pos[HALO:, :1])
+    for h in range(q_part.shape[1] // HD):
+        cols = slice(h * HD, (h + 1) * HD)
+        q = q_part[queries_at, cols].astype(jnp.float32)
+        for k in range(n_t - 1):
+            q += q_recv[k, :, cols].astype(jnp.float32)
+        q_rot = turn(q * inverse[HALO:], cosine[HALO:], sine[HALO:]).astype(jnp.bfloat16)
+        scores = lax.dot_general(
+            q_rot, k_rot, (((1,), (1,)), ((), ())), preferred_element_type=jnp.float32
+        ) * (1.0 / math.sqrt(HD))
+        scores = jnp.where(allowed, scores, -jnp.inf)
+        exponent = jnp.exp(scores - jnp.max(scores, axis=1, keepdims=True))
+        weights = (exponent / jnp.sum(exponent, axis=1, keepdims=True)).astype(jnp.bfloat16)
+        ctx[queries_at, cols] = jnp.dot(
+            weights, values, preferred_element_type=jnp.float32
+        ).astype(jnp.bfloat16)
+
+    gathers = []
+    for k in range(1, n_t):
+        at = ctx.at[queries_at]
+        gathers.append(send(at, at, (me, t_at(k))))
+    own_o.wait()
+    for copy in o_last:
+        copy.wait_recv()
+    for copy in gathers:
+        copy.wait_recv()
+
+    def out_tile(i, carry):
+        at = pl.ds(aligned(i, tile), tile)
+        total = packed[:, at].astype(jnp.float32)
+        for u in range(n_t):
+            total += jnp.dot(
+                ctx[:, u * o_rows : (u + 1) * o_rows],
+                obuf[u, :, at],
+                preferred_element_type=jnp.float32,
+            )
+        out[:, at] = jnp.where(valid_buf[:, :1] > 0.0, total, 0.0).astype(jnp.bfloat16)
+        return carry
+
+    lax.fori_loop(0, tiles, out_tile, 0)
+    for copy in started:
+        copy.wait_send()
+
+
+def fused_body(rollout, lengths, packing, norm_gain, query_weight, keyval_weight, out_weight):
+    n_dp, n_t = lax.axis_size("dp"), lax.axis_size("tensor")
+    length, feat = rollout.shape
+    per_source = lengths.shape[1]
+    most = length // per_source
+    qd, kd = query_weight.shape[1], keyval_weight.shape[1]
+    quarter = feat // 4
+    kv = keyval_weight.reshape(n_t, 4, quarter, kd)
+    w = jnp.concatenate(
+        [query_weight.reshape(n_t, feat, qd), jnp.concatenate([kv[:, i] for i in range(4)], axis=2)],
+        axis=1,
+    )
+    pk = packing.astype(jnp.float32)
+    flat = lengths.reshape(-1).astype(jnp.float32)
+    frequency = np.float32(rope_base) ** (-np.arange(HD // 2, dtype=np.float32) * 2.0 / HD)
+    angles = np.arange(most, dtype=np.float32)[:, None] * frequency[None, :].astype(np.float32)
+    cos_tab = np.concatenate([np.cos(angles)] * 2, axis=1).astype(np.float32)
+    sin_tab = np.concatenate([-np.sin(angles), np.sin(angles)], axis=1).astype(np.float32)
+    rows = length // n_t
+    chips = n_dp // CORES
+    copies = 2 * (n_t - 1) * (1 + chips - 1 + chips) + (n_dp - 1) + 3 * (n_t - 1)
+    vmem = pl.BlockSpec(memory_space=pltpu.VMEM)
+    hbm = pl.BlockSpec(memory_space=pl.ANY)
+    bf, f32 = jnp.bfloat16, jnp.float32
+    return pl.pallas_call(
+        functools.partial(fused_kernel, (n_dp, n_t, length, feat, per_source)),
+        out_shape=jax.ShapeDtypeStruct((length, feat), bf),
+        in_specs=[vmem] * 8 + [hbm] * 2,
+        out_specs=vmem,
+        scratch_shapes=[
+            pltpu.VMEM(w.shape, bf),
+            pltpu.VMEM((n_t, out_weight.shape[0], feat), bf),
+            pltpu.VMEM((length, feat), bf),
+            pltpu.VMEM((length, feat), bf),
+            pltpu.VMEM((length, feat), bf),
+            pltpu.VMEM((length, feat), bf),
+            pltpu.VMEM((length, n_t * qd), bf),
+            pltpu.VMEM((length + HALO, 3 * HD), bf),
+            pltpu.VMEM((n_t, length, HD), f32),
+            pltpu.VMEM((n_t - 1, rows, n_t * qd), bf),
+            pltpu.VMEM((n_t - 1, rows + HALO, 3 * HD), bf),
+            pltpu.VMEM((length, n_t * qd), bf),
+            pltpu.VMEM((length + HALO, HD), f32),
+            pltpu.VMEM((length, HD), f32),
+            pltpu.SemaphoreType.DMA((copies,)),
+            pltpu.SemaphoreType.DMA((copies,)),
+            pltpu.SemaphoreType.DMA((2,)),
+        ],
+        compiler_params=pltpu.CompilerParams(
+            collective_id=0, has_side_effects=True, vmem_limit_bytes=48 * 1024 * 1024
+        ),
+    )(
+        pk[:, None], pk[None, :], flat[:, None], flat[None, :], norm_gain[None, :],
+        jnp.asarray(cos_tab), jnp.asarray(sin_tab), rollout, w, out_weight,
+    )
+
+
+def body(rollout, lengths, packing, norm_gain, query_weight, keyval_weight, out_weight):
+    n_dp, n_t = lax.axis_size("dp"), lax.axis_size("tensor")
+    length, feat = rollout.shape
+    qd, kd = query_weight.shape[1], keyval_weight.shape[1]
+    fits = (
+        kd * n_t == 2 * HD
+        and n_t == 4
+        and qd == 4 * kd
+        and n_dp % CORES == 0
+        and length % (n_t * HALO) == 0
+        and packing.shape[0] == length
+        and (length // n_dp) % HALO == 0
+        and feat % 512 == 0
+        and lengths.shape[1] % n_dp == 0
+    )
+    chosen = fused_body if fits else plain_body
+    return chosen(rollout, lengths, packing, norm_gain, query_weight, keyval_weight, out_weight)
+
+
 def solution(mesh):
     in_specs = (
         P("dp", "tensor"),

time: 228 us -> 88.6 us (0.39)
  waiting for transfers between devices: 125 us -> 0 us
  Pallas kernels: 0 us -> 71.2 us
  other arithmetic: 51.9 us -> 5.63 us
  blocking collectives: 13.4 us -> 0 us
  between operations: 13.4 us -> 0.1 us
  matrix products: 10.3 us -> 0 us
  local copies, waits for them, and re-layouts: 13.2 us -> 10.3 us
    pallas_call x0 -> x1, Pallas kernels: none -> 71.2 us  [fused_body(): pl.pallas_call(functools.partial(fused_kernel, (n_dp, n_t, length, feat,...]
    all_gather x2 -> x0, waiting for transfers between devices: 65.2 us -> none  [the longest x1 64.9 us: body(): lax.all_gather(packed, 'tensor', axis=1, tiled=True).astype(jnp.float32)]
    reduce_scatter x1 -> x0, waiting for transfers between devices: 59.1 us -> none  [body(): lax.psum_scatter(partial_sum.astype(jnp.bfloat16), 'tensor', scatter_dime...]
    select_n x5 -> x0, other arithmetic: 23.1 us -> none  [the longest x1 20.2 us: body(): jnp.take(source_start.reshape(-1), response)]
    convert_element_type x3 -> x2, other arithmetic: 22.9 us -> 0.01 us  [the longest x1 0.01 us: fused_body(): pk = packing.astype(jnp.float32)]
    all_gather x1 -> x0, blocking collectives: 13.4 us -> none  [body(): keyval_all = lax.all_gather(keyval_share, 'tensor', axis=1, tiled=True)]
    gather x7 -> x0, local copies, waits for them, and re-layouts: 12 us -> none  [the longest x1 6.47 us: body(): jnp.take(portion, jnp.clip(global_row, 0, portion.shape[0] - 1), axis=0)]
    dot_general x5 -> x0, matrix products: 9.03 us -> none  [the longest x1 2.67 us: body(): jnp.dot(context, out_weight, preferred_element_type=jnp.float32)]
  transfers between devices with their start and end apart: 3 -> 0, of which waited for: 3 -> 0; matrix products, arithmetic and copies ran while one was open for 22% -> 0% of each run, Pallas kernels for 0% -> 0%
where the time goes in v1:
time: 88.6 us; the launch traced here: 87.2 us
  Pallas kernels  71.2 us (80%)
  local copies, waits for them, and re-layouts  10.3 us (12%)
  other arithmetic  5.63 us (6%)
    pallas_call x1, Pallas kernels, fused_body(): pl.pallas_call(functools.partial(fused_kernel, (n_dp, n_t, length, feat,...  71.2 us
    unnamed x19, local copies, waits for them, and re-layouts  6.49 us
    concatenate x1, other arithmetic, fused_body(): jnp.concatenate([query_weight.reshape(n_t, feat, qd), jnp.concatenate([kv...  5.62 us
    reshape x1, local copies, waits for them, and re-layouts, fused_body(): kv = keyval_weight.reshape(n_t, 4, quarter, kd)  2.31 us

profile of v1, /device:TPU:0, one launch (start us, length us, event | category | flops | bytes accessed | tf_op | source)
XLA Modules:
  0.0 87.2 jit_solution(13896080459826639691)
XLA Ops:
  0.0 2.3 %reshape.30 = bf16[4,4,384,64]{2,1,0,3:T(4,128)(2,1)S(1)} reshape(bf16[6144,64]{0,1:T(8,128)(2,1)} %param.14) | data formatting | bytes 1572864 | tf_op jit(solution)/shard_map/reshape | solution.py:407
  2.3 1.1 %fusion = (bf16[4,1,384,64]{2,1,0,3:T(2,128)(2,1)S(1)}, bf16[4,1,384,64]{2,1,0,3:T(2,128)(2,1)S(1)}, bf16[4,1,384,64]{2,1,0,3:T(2,128)(2,1)S(1)}, bf16[4,1,384,64]{2,1,0,3:T(2,128)(2,1)S(1)}) fusion(bf16[4,4,384,64]{2,1,0,3:T(4,128)(2,1)S(1)} %reshape.30), kind=kLoop, calls=%fused_computation.1 | loop fusion | bytes 1572864 | tf_op jit(solution)/shard_map/slice | solution.py:409
  3.5 1.1 %copy.16 = bf16[4,1,384,64]{3,2,0,1:T(8,128)(2,1)} copy(bf16[4,1,384,64]{2,1,0,3:T(2,128)(2,1)S(1)} %get-tuple-element.5) | data formatting | bytes 393216
  4.6 1.1 %copy.17 = bf16[4,1,384,64]{3,2,0,1:T(8,128)(2,1)} copy(bf16[4,1,384,64]{2,1,0,3:T(2,128)(2,1)S(1)} %get-tuple-element.7) | data formatting | bytes 393216
  5.7 1.1 %copy.18 = bf16[4,1,384,64]{3,2,0,1:T(8,128)(2,1)} copy(bf16[4,1,384,64]{2,1,0,3:T(2,128)(2,1)S(1)} %get-tuple-element.6) | data formatting | bytes 393216
  6.8 1.1 %copy.19 = bf16[4,1,384,64]{3,2,0,1:T(8,128)(2,1)} copy(bf16[4,1,384,64]{2,1,0,3:T(2,128)(2,1)S(1)} %get-tuple-element.8) | data formatting | bytes 393216
  7.9 0.0 copy-start.5
  7.9 0.0 copy-start.6
  7.9 0.0 copy-start
  7.9 0.0 copy-start.2
  7.9 0.0 copy-start.3
  7.9 0.0 copy-start.4
  7.9 5.6 %maximum_maximum_fusion.w_in = bf16[4,1920,256]{2,1,0:T(8,128)(2,1)} fusion(bf16[4,384,64]{2,1,0:T(8,128)(2,1)} %bitcast.17, bf16[4,384,64]{2,1,0:T(8,128)(2,1)} %bitcast.16, bf16[4,384,64]{2,1,0:T(8,128)(2,1)} %bitcast.15, bf16[4,384,64]{2,1,0:T(8,128)(2,1)} %bitcast.14, bf16[4,1536,256]{2,1,0:T(8,128)(2,1)} %bitcast.13), kind=kLoop, calls=%fused_computation | loop fusion | flops 19660800 | bytes 7864320 | tf_op jit(solution)/shard_map/concatenate | solution.py:408
  13.6 0.0 copy-done.5
  13.6 0.1 convert_element_type.30.len_col
  13.7 0.0 copy-done.6
  13.7 0.1 copy.14.pk_col
  13.9 0.1 convert_element_type.29.len_row
  13.9 0.0 copy-done
  13.9 0.0 copy-done.2
  14.0 0.0 copy-done.3
  14.0 0.0 copy-done.4
  14.0 0.0 copy-start.1
  14.0 1.1 %copy-done.1 = bf16[256,1536]{1,0:T(8,128)(2,1)S(1)} copy-done((bf16[256,1536]{1,0:T(8,128)(2,1)S(1)}, bf16[256,1536]{1,0:T(8,128)(2,1)}, u32[]{:S(2)}) %copy-start.1) | copy-done | bytes 786456
  15.1 71.2 %shard_map.91 = bf16[256,1536]{1,0:T(8,128)(2,1)S(1)} custom-call(f32[256,1]{1,0:T(8,128)S(1)} %copy.14.pk_col, f32[1,256]{1,0:T(1,128)S(1)} %bitcast.12, f32[256,1]{1,0:T(8,128)S(1)} %convert_element_type.30.len_col, f32[1,256]{1,0:T(1,128)S(1)} %convert_element_type.29.len_row, f32[1,6144]{1,0:T(1,128)S(1)} %bitcast.10, f32[8,128]{1,0:T(8,128)S(1)} %copy-done.3, ...), custom_call_target="tpu_custom_call" | custom-call | tf_op jit(solution)/shard_map/pallas_call | solution.py:424
  86.3 0.9 %copy.21 = bf16[256,1536]{1,0:T(8,128)(2,1)} copy(bf16[256,1536]{1,0:T(8,128)(2,1)S(1)} %shard_map.91) | data formatting | bytes 1572864
  (2 shorter events, 0.0 us)
Async XLA Ops:
  7.9 5.7 %copy-start.5 = (s32[8,32]{1,0:T(8,128)S(1)}, s32[8,32]{1,0:T(8,128)}, u32[]{:S(2)}) copy-start(s32[8,32]{1,0:T(8,128)} %param.10) | copy-start | bytes 3076
  7.9 5.8 %copy-start.6 = (s32[256]{0:T(256)S(1)}, s32[256]{0:T(256)}, u32[]{:S(2)}) copy-start(s32[256]{0:T(256)} %param.11) | copy-start | bytes 3076
  7.9 6.0 %copy-start = (bf16[256,6144]{1,0:T(8,128)(2,1)S(1)}, bf16[256,6144]{1,0:T(8,128)(2,1)}, u32[]{:S(2)}) copy-start(bf16[256,6144]{1,0:T(8,128)(2,1)} %o_in.1) | copy-start | bytes 9437188
  7.9 6.0 %copy-start.2 = (f32[6144]{0:T(1024)S(1)}, f32[6144]{0:T(1024)}, u32[]{:S(2)}) copy-start(f32[6144]{0:T(1024)} %param.12) | copy-start | bytes 73732
  7.9 6.0 %copy-start.3 = (f32[8,128]{1,0:T(8,128)S(1)}, f32[8,128]{1,0:T(8,128)}, u32[]{:S(2)}) copy-start(f32[8,128]{1,0:T(8,128)} %constant.4.clone.cos_tab) | copy-start | bytes 12292
  7.9 6.0 %copy-start.4 = (f32[8,128]{1,0:T(8,128)S(1)}, f32[8,128]{1,0:T(8,128)}, u32[]{:S(2)}) copy-start(f32[8,128]{1,0:T(8,128)} %constant.5.clone.sin_tab) | copy-start | bytes 12292
  14.0 1.1 %copy-start.1 = (bf16[256,1536]{1,0:T(8,128)(2,1)S(1)}, bf16[256,1536]{1,0:T(8,128)(2,1)}, u32[]{:S(2)}) copy-start(bf16[256,1536]{1,0:T(8,128)(2,1)} %roll_in.1) | copy-start | bytes 2359300

commit v2 on v1

--- a/solution.py
+++ b/solution.py
@@ -108,20 +108,21 @@
 
 
 def fused_kernel(
-    cfg, pk_col, pk_row, len_col, len_row, gain, cos_tab, sin_tab, roll_in, w_in, o_in, out,
-    wbuf, obuf, sendb, recvb, packed, scaled, q_part, kv_part, kv_acc, q_recv, kv_recv, ctx,
+    cfg, pk_hbm, len_hbm, gain_hbm, tab_hbm, roll_hbm, w_in, k_in, o_in, out,
+    pk_buf, len_buf, gain, tab, wbuf, kbuf, obuf, roll_in, sendb, recvb, packed, scaled, q_part, kv_part, q_recv, kv_recv, ctx,
     pos_buf, valid_buf, send_sems, recv_sems, local_sems,
 ):
     n_dp, n_t, length, feat, per_source = cfg
     chips = n_dp // CORES
-    w_sub = wbuf.shape[1] // n_dp
+    w_sub = feat // n_dp
+    kd = k_in.shape[0]
+    k_rows, k_cols = kd // chips, feat // CORES
     o_rows = o_in.shape[0]
     o_sub = o_rows // n_dp
     block = length // n_dp
     most = length // per_source
     rows = length // n_t
-    qd = w_in.shape[2]
-    quarter = feat // 4
+    qd = w_in.shape[1]
     me = lax.axis_index("dp")
     t = lax.axis_index("tensor")
     core = lax.rem(me, CORES)
@@ -133,6 +134,21 @@
 
     def chip_at(k):
         return lax.rem(chip + k, chips) * CORES + core
+
+    small = [
+        pltpu.make_async_copy(source, target, local_sems.at[4 + i])
+        for i, (source, target) in enumerate(
+            (
+                (pk_hbm, pk_buf),
+                (len_hbm, len_buf),
+                (gain_hbm.at[:, pl.ds(aligned(t, feat), feat)], gain),
+                (tab_hbm, tab),
+            )
+        )
+    ]
+    load = pltpu.make_async_copy(roll_hbm, roll_in, local_sems.at[2])
+    for copy in [*small, load]:
+        copy.start()
 
     barrier = pltpu.get_barrier_semaphore()
     for k in range(1, n_dp):
@@ -159,21 +175,48 @@
         started.append(copy)
         return copy
 
-    w_first, o_first = {}, {}
+    def w_at(u, h, c):
+        return wbuf.at[u, pl.ds(aligned(h * CORES + c, w_sub), w_sub)]
+
+    def k_at(u, h, c):
+        return kbuf.at[
+            pl.ds(aligned(u * chips + h, k_rows), k_rows), pl.ds(aligned(c, k_cols), k_cols)
+        ]
+
+    def o_at(u, h, c):
+        return obuf.at[u, pl.ds(aligned(h * CORES + c, o_sub), o_sub)]
+
+    w_first, k_first, o_first = {}, {}, {}
+    for k in range(1, n_t):
+        to = t_at(k)
+        k_first[k] = send(
+            k_in.at[
+                pl.ds(aligned(chip, k_rows), k_rows),
+                pl.ds(aligned(to * CORES + core, k_cols), k_cols),
+            ],
+            k_at(t, chip, core),
+            (me, to),
+        )
     for k in range(1, n_t):
         to = t_at(k)
         w_first[k] = send(
-            w_in.at[to, pl.ds(aligned(me, w_sub), w_sub)],
-            wbuf.at[t, pl.ds(aligned(me, w_sub), w_sub)],
-            (me, to),
-        )
-    own_w = pltpu.make_async_copy(w_in.at[t], wbuf.at[t], local_sems.at[0])
+            w_in.at[pl.ds(aligned(to * n_dp + me, w_sub), w_sub)], w_at(t, chip, core), (me, to)
+        )
+    own_w = pltpu.make_async_copy(
+        w_in.at[pl.ds(aligned(t, feat), feat)], wbuf.at[t], local_sems.at[0]
+    )
     own_w.start()
+    own_k = pltpu.make_async_copy(
+        k_in.at[:, pl.ds(aligned(t, feat), feat)],
+        kbuf.at[pl.ds(aligned(t, kd), kd)],
+        local_sems.at[3],
+    )
+    own_k.start()
     for k in range(1, n_t):
         to = t_at(k)
         o_first[k] = send(
             o_in.at[pl.ds(aligned(me, o_sub), o_sub), pl.ds(aligned(to, feat), feat)],
-            obuf.at[t, pl.ds(aligned(me, o_sub), o_sub)],
+            o_at(t, chip, core),
             (me, to),
         )
     own_o = pltpu.make_async_copy(
@@ -191,8 +234,19 @@
         return jnp.sum(jnp.where(mask, value, 0.0), axis=axis, keepdims=True)
 
     same = part(down, per_source) == part(across, per_source)
-    len_c, len_r = len_col[...], len_row[...]
-    pk_c, pk_r = pk_col[...], pk_row[...]
+    diagonal = down == across
+    for copy in small:
+        copy.wait()
+    len_all = len_buf[...].astype(jnp.float32)
+    source_of = part(down[:, :1], per_source)
+    table = jnp.zeros((length, per_source), jnp.float32)
+    for i in range(n_dp):
+        table = jnp.where(source_of == float(i), len_all[i : i + 1, :], table)
+    within = down[:, :per_source] - source_of * per_source
+    len_c = pick(across[:, :per_source] == within, table, 1)
+    len_r = pick(diagonal, len_c, 0)
+    pk_r = pk_buf[...].astype(jnp.float32)
+    pk_c = pick(diagonal, pk_r, 1)
     src_start = pick(same & (across < down), len_r, 1)
     chosen = down == pk_r
     q_len_r = pick(chosen, len_c, 0)
@@ -233,6 +287,7 @@
         ).astype(jnp.bfloat16)
         return carry
 
+    load.wait()
     lax.fori_loop(0, tiles, send_tile, 0)
 
     rows_of = {}
@@ -246,28 +301,23 @@
     keep = pl.ds(aligned(me, block), block)
     recvb[keep, :] = sendb[keep, :]
 
-    def spread(buf, first, sub):
-        hops = {}
-        for j in range(1, n_t):
-            first[j].wait_recv()
-            at = buf.at[t_at(n_t - j), pl.ds(aligned(me, sub), sub)]
-            for k in range(1, chips):
-                hops[j, k] = send(at, at, (chip_at(k), t))
-        return hops
-
-    def share(buf, hops, sub):
+    def spread(at, first, j):
+        first[j].wait_recv()
+        ref = at(t_at(n_t - j), chip, core)
+        return [send(ref, ref, (chip_at(k), t)) for k in range(1, chips)]
+
+    def share(at, hops, j):
         last = []
         for k in range(chips):
-            for j in range(1, n_t):
-                if k:
-                    hops[j, k].wait_recv()
-                at = buf.at[
-                    t_at(n_t - j), pl.ds(aligned(chip_at(chips - k if k else 0), sub), sub)
-                ]
-                last.append(send(at, at, (partner, t)))
+            if k:
+                hops[k - 1].wait_recv()
+            ref = at(t_at(n_t - j), lax.rem(chip + chips - k, chips), core)
+            last.append(send(ref, ref, (partner, t)))
         return last
 
-    w_hops = spread(wbuf, w_first, w_sub)
+    others = range(1, n_t)
+    k_hops = {j: spread(k_at, k_first, j) for j in others}
+    w_hops = {1: spread(w_at, w_first, 1)}
 
     for k in range(1, n_dp):
         rows_of[k].wait_recv()
@@ -276,7 +326,7 @@
         at = pl.ds(aligned(i, tile), tile)
         x = jnp.dot(take_recv, recvb[:, at], preferred_element_type=jnp.float32)
         packed[:, at] = x.astype(jnp.bfloat16)
-        g = gain[:, pl.ds(pl.multiple_of(t * feat + i * tile, tile), tile)]
+        g = gain[:, at]
         scaled[:, at] = (x * g).astype(jnp.bfloat16)
         return total + jnp.sum(x * x, axis=1, keepdims=True)
 
@@ -288,48 +338,53 @@
         lane < HD // 2, jnp.broadcast_to(high, (length, HD)), jnp.broadcast_to(squares - high, (length, HD))
     ).astype(jnp.bfloat16)
 
-    o_hops = spread(obuf, o_first, o_sub)
-    w_last = share(wbuf, w_hops, w_sub)
+    shares = []
+
+    def reduce_rows(part_ref, recv_ref, extra, cols):
+        for k in others:
+            to = t_at(k)
+            shares.append(
+                send(
+                    part_ref.at[pl.ds(aligned(to, rows), rows + extra), cols],
+                    recv_ref.at[k - 1, :, cols],
+                    (me, to),
+                )
+            )
+
+    def project(j):
+        u = t_at(n_t - j)
+        cols = pl.ds(aligned(u, qd), qd)
+        q_part[:, cols] = jnp.dot(
+            scaled[...], wbuf[u], preferred_element_type=jnp.float32
+        ).astype(jnp.bfloat16)
+        reduce_rows(q_part, q_recv, 0, cols)
+
     own_w.wait()
-    for copy in w_last:
+    own_k.wait()
+    reduce_rows(kv_part, kv_recv, HALO, pl.ds(2 * HD, HD))
+    project(n_t)
+    for j in others[1:]:
+        w_hops[j] = spread(w_at, w_first, j)
+    k_last = [copy for j in others for copy in share(k_at, k_hops[j], j)]
+    for copy in k_last:
         copy.wait_recv()
-
-    def project(u, carry):
-        x = scaled[...]
-        q_part[:, pl.ds(aligned(u, qd), qd)] = jnp.dot(
-            x, wbuf[u, :feat, :], preferred_element_type=jnp.float32
-        ).astype(jnp.bfloat16)
-        w = wbuf[u, feat:, :]
-        y = jnp.dot(x[:, :quarter], w, preferred_element_type=jnp.float32)
-        for i in range(1, 4):
-            z = jnp.dot(
-                x[:, i * quarter : (i + 1) * quarter], w, preferred_element_type=jnp.float32
-            )
-            y += pltpu.roll(z, qd - i * (qd // 4), 1)
-        kv_acc[u] = y[:, :HD]
-        return carry
-
-    lax.fori_loop(0, n_t, project, 0)
-    for i in range(2):
-        kv_part[HALO:, i * HD : (i + 1) * HD] = jnp.where(
-            lane < HD // 2, kv_acc[2 * i], pltpu.roll(kv_acc[2 * i + 1], HD // 2, 1)
-        ).astype(jnp.bfloat16)
-
-    shares = []
-    for k in range(1, n_t):
-        to = t_at(k)
-        shares.append(
-            send(
-                kv_part.at[pl.ds(aligned(to, rows), rows + HALO)], kv_recv.at[k - 1], (me, to)
-            )
-        )
-        shares.append(
-            send(q_part.at[pl.ds(aligned(to, rows), rows)], q_recv.at[k - 1], (me, to))
-        )
-    o_last = share(obuf, o_hops, o_sub)
-
+    kv_part[HALO:, : 2 * HD] = lax.dot_general(
+        scaled[...], kbuf[...], (((1,), (1,)), ((), ())), preferred_element_type=jnp.float32
+    ).astype(jnp.bfloat16)
+    reduce_rows(kv_part, kv_recv, HALO, pl.ds(0, 2 * HD))
+    w_last = share(w_at, w_hops[1], 1)
+    o_hops = {}
+    for j in others:
+        if j + 1 in w_hops:
+            following = share(w_at, w_hops[j + 1], j + 1)
+        for copy in w_last:
+            copy.wait_recv()
+        w_last = following
+        project(j)
+        o_hops[j] = spread(o_at, o_first, j)
     for copy in shares:
         copy.wait_recv()
+
     keys_at = pl.ds(aligned(t, rows), rows + HALO)
     queries_at = pl.ds(aligned(t, rows), rows)
     kv = kv_part[keys_at, :].astype(jnp.float32)
@@ -344,8 +399,8 @@
     sine = jnp.zeros((rows + HALO, HD), jnp.float32)
     for m in range(most):
         at_m = pos == float(m)
-        cosine = jnp.where(at_m, cos_tab[m : m + 1, :], cosine)
-        sine = jnp.where(at_m, sin_tab[m : m + 1, :], sine)
+        cosine = jnp.where(at_m, tab[m : m + 1, :], cosine)
+        sine = jnp.where(at_m, tab[most + m : most + m + 1, :], sine)
 
     def turn(v, c, s):
         return v * c + pltpu.roll(v, HD // 2, 1) * s
@@ -354,7 +409,9 @@
     q_down = lax.broadcasted_iota(jnp.int32, (rows, rows + HALO), 0).astype(jnp.float32)
     k_across = lax.broadcasted_iota(jnp.int32, (rows, rows + HALO), 1).astype(jnp.float32) - HALO
     allowed = (k_across <= q_down) & (k_across >= q_down - pos[HALO:, :1])
-    for h in range(q_part.shape[1] // HD):
+    gathers = []
+    heads = q_part.shape[1] // HD
+    for h in range(heads):
         cols = slice(h * HD, (h + 1) * HD)
         q = q_part[queries_at, cols].astype(jnp.float32)
         for k in range(n_t - 1):
@@ -369,11 +426,12 @@
         ctx[queries_at, cols] = jnp.dot(
             weights, values, preferred_element_type=jnp.float32
         ).astype(jnp.bfloat16)
-
-    gathers = []
-    for k in range(1, n_t):
-        at = ctx.at[queries_at]
-        gathers.append(send(at, at, (me, t_at(k))))
+        if (h + 1) % (heads // n_t) == 0:
+            at = ctx.at[queries_at, pl.ds((h + 1 - heads // n_t) * HD, heads // n_t * HD)]
+            for k in others:
+                gathers.append(send(at, at, (me, t_at(k))))
+
+    o_last = [copy for j in others for copy in share(o_at, o_hops[j], j)]
     own_o.wait()
     for copy in o_last:
         copy.wait_recv()
@@ -403,39 +461,36 @@
     per_source = lengths.shape[1]
     most = length // per_source
     qd, kd = query_weight.shape[1], keyval_weight.shape[1]
-    quarter = feat // 4
-    kv = keyval_weight.reshape(n_t, 4, quarter, kd)
-    w = jnp.concatenate(
-        [query_weight.reshape(n_t, feat, qd), jnp.concatenate([kv[:, i] for i in range(4)], axis=2)],
-        axis=1,
-    )
-    pk = packing.astype(jnp.float32)
-    flat = lengths.reshape(-1).astype(jnp.float32)
     frequency = np.float32(rope_base) ** (-np.arange(HD // 2, dtype=np.float32) * 2.0 / HD)
     angles = np.arange(most, dtype=np.float32)[:, None] * frequency[None, :].astype(np.float32)
     cos_tab = np.concatenate([np.cos(angles)] * 2, axis=1).astype(np.float32)
     sin_tab = np.concatenate([-np.sin(angles), np.sin(angles)], axis=1).astype(np.float32)
     rows = length // n_t
     chips = n_dp // CORES
-    copies = 2 * (n_t - 1) * (1 + chips - 1 + chips) + (n_dp - 1) + 3 * (n_t - 1)
+    copies = 3 * (n_t - 1) * (1 + chips - 1 + chips) + (n_dp - 1) + (2 + 2 * n_t) * (n_t - 1)
     vmem = pl.BlockSpec(memory_space=pltpu.VMEM)
     hbm = pl.BlockSpec(memory_space=pl.ANY)
     bf, f32 = jnp.bfloat16, jnp.float32
     return pl.pallas_call(
         functools.partial(fused_kernel, (n_dp, n_t, length, feat, per_source)),
         out_shape=jax.ShapeDtypeStruct((length, feat), bf),
-        in_specs=[vmem] * 8 + [hbm] * 2,
+        in_specs=[hbm] * 8,
         out_specs=vmem,
         scratch_shapes=[
-            pltpu.VMEM(w.shape, bf),
+            pltpu.VMEM((1, packing.shape[0]), jnp.int32),
+            pltpu.VMEM(lengths.shape, jnp.int32),
+            pltpu.VMEM((1, feat), f32),
+            pltpu.VMEM((2 * most, HD), f32),
+            pltpu.VMEM((n_t, feat, qd), bf),
+            pltpu.VMEM((n_t * kd, feat), bf),
             pltpu.VMEM((n_t, out_weight.shape[0], feat), bf),
+            pltpu.VMEM((length, feat), bf),
             pltpu.VMEM((length, feat), bf),
             pltpu.VMEM((length, feat), bf),
             pltpu.VMEM((length, feat), bf),
             pltpu.VMEM((length, feat), bf),
             pltpu.VMEM((length, n_t * qd), bf),
             pltpu.VMEM((length + HALO, 3 * HD), bf),
-            pltpu.VMEM((n_t, length, HD), f32),
             pltpu.VMEM((n_t - 1, rows, n_t * qd), bf),
             pltpu.VMEM((n_t - 1, rows + HALO, 3 * HD), bf),
             pltpu.VMEM((length, n_t * qd), bf),
@@ -443,14 +498,15 @@
             pltpu.VMEM((length, HD), f32),
             pltpu.SemaphoreType.DMA((copies,)),
             pltpu.SemaphoreType.DMA((copies,)),
-            pltpu.SemaphoreType.DMA((2,)),
+            pltpu.SemaphoreType.DMA((8,)),
         ],
         compiler_params=pltpu.CompilerParams(
-            collective_id=0, has_side_effects=True, vmem_limit_bytes=48 * 1024 * 1024
+            collective_id=0, has_side_effects=True, vmem_limit_bytes=60 * 1024 * 1024
         ),
     )(
-        pk[:, None], pk[None, :], flat[:, None], flat[None, :], norm_gain[None, :],
-        jnp.asarray(cos_tab), jnp.asarray(sin_tab), rollout, w, out_weight,
+        packing[None, :], lengths, norm_gain[None, :],
+        jnp.asarray(np.concatenate([cos_tab, sin_tab])), rollout, query_weight,
+        keyval_weight.T, out_weight,
     )
 
 
@@ -461,7 +517,8 @@
     fits = (
         kd * n_t == 2 * HD
         and n_t == 4
-        and qd == 4 * kd
+        and kd % (HALO * n_dp // CORES) == 0
+        and feat % (128 * CORES) == 0
         and n_dp % CORES == 0
         and length % (n_t * HALO) == 0
         and packing.shape[0] == length

time: 88.6 us -> 62.7 us (0.71); the launches traced: 87.2 us -> 62.6 us
  Pallas kernels: 71.2 us -> 60.5 us
  local copies, waits for them, and re-layouts: 10.3 us -> 2.06 us
  other arithmetic: 5.63 us -> 0 us
    pallas_call x1, Pallas kernels: 71.2 us -> 60.5 us  [fused_body(): pl.pallas_call(functools.partial(fused_kernel, (n_dp, n_t, length, feat,...]
    concatenate x1 -> x0, other arithmetic: 5.62 us -> none  [fused_body(): jnp.concatenate([query_weight.reshape(n_t, feat, qd), jnp.concatenate([kv...]
    unnamed x19 -> x1, local copies, waits for them, and re-layouts: 6.49 us -> 2.06 us
    reshape x1 -> x0, local copies, waits for them, and re-layouts: 2.31 us -> none  [fused_body(): kv = keyval_weight.reshape(n_t, 4, quarter, kd)]
    slice x1 -> x0, local copies, waits for them, and re-layouts: 1.13 us -> none  [fused_body(): kv[:, i]]
where the time goes in v2:
time: 62.7 us; the launch traced here: 62.6 us
  Pallas kernels  60.5 us (96%)
  local copies, waits for them, and re-layouts  2.06 us (3%)
    pallas_call x1, Pallas kernels, fused_body(): pl.pallas_call(functools.partial(fused_kernel, (n_dp, n_t, length, feat,...  60.5 us
    unnamed x1, local copies, waits for them, and re-layouts  2.06 us

profile of v2, /device:TPU:0, one launch (start us, length us, event | category | flops | bytes accessed | tf_op | source)
XLA Modules:
  0.0 62.6 jit_solution(13465847414951764553)
XLA Ops:
  0.0 60.5 %shard_map.82 = bf16[256,1536]{1,0:T(8,128)(2,1)} custom-call(s32[1,256]{1,0:T(1,128)} %bitcast.5, s32[8,32]{1,0:T(8,128)} %len_hbm.1, f32[1,6144]{1,0:T(1,128)} %bitcast.4, f32[16,128]{1,0:T(8,128)} %constant.2.clone.tab_hbm, bf16[256,1536]{1,0:T(8,128)(2,1)} %roll_hbm.1, bf16[6144,256]{1,0:T(8,128)(2,1)} %w_in.1, bf16[64,6144]{1,0:T(8,128)(2,1)} %bitcast.3, ...), custom_call_target="tpu_custom_call" | custom-call | tf_op jit(solution)/shard_map/pallas_call | solution.py:474
  60.5 2.1 %copy.10 = bf16[256,1536]{1,0:T(8,128)(2,1)} copy(bf16[256,1536]{1,0:T(8,128)(2,1)} %shard_map.82) | data formatting | bytes 1572864

commit v3 on v2

--- a/solution.py
+++ b/solution.py
@@ -110,7 +110,7 @@
 def fused_kernel(
     cfg, pk_hbm, len_hbm, gain_hbm, tab_hbm, roll_hbm, w_in, k_in, o_in, out,
     pk_buf, len_buf, gain, tab, wbuf, kbuf, obuf, roll_in, sendb, recvb, packed, scaled, q_part, kv_part, q_recv, kv_recv, ctx,
-    pos_buf, valid_buf, send_sems, recv_sems, local_sems,
+    pos_buf, valid_buf, acc, sq_part, sq_recv, send_sems, recv_sems, local_sems,
 ):
     n_dp, n_t, length, feat, per_source = cfg
     chips = n_dp // CORES
@@ -331,13 +331,8 @@
         return total + jnp.sum(x * x, axis=1, keepdims=True)
 
     squares = lax.fori_loop(0, tiles, pack_tile, jnp.zeros((length, 1), jnp.float32))
-    lane = lax.broadcasted_iota(jnp.int32, (length, HD), 1)
-    high = squares.astype(jnp.bfloat16).astype(jnp.float32)
-    kv_part[:HALO, :] = jnp.zeros((HALO, 3 * HD), jnp.bfloat16)
-    kv_part[HALO:, 2 * HD :] = jnp.where(
-        lane < HD // 2, jnp.broadcast_to(high, (length, HD)), jnp.broadcast_to(squares - high, (length, HD))
-    ).astype(jnp.bfloat16)
-
+    kv_part[:HALO, :] = jnp.zeros((HALO, 2 * HD), jnp.bfloat16)
+    sq_part[...] = jnp.broadcast_to(pick(diagonal, squares, 0), (8, length))
     shares = []
 
     def reduce_rows(part_ref, recv_ref, extra, cols):
@@ -361,7 +356,8 @@
 
     own_w.wait()
     own_k.wait()
-    reduce_rows(kv_part, kv_recv, HALO, pl.ds(2 * HD, HD))
+    for k in others:
+        shares.append(send(sq_part, sq_recv.at[k - 1], (me, t_at(k))))
     project(n_t)
     for j in others[1:]:
         w_hops[j] = spread(w_at, w_first, j)
@@ -390,7 +386,11 @@
     kv = kv_part[keys_at, :].astype(jnp.float32)
     for k in range(n_t - 1):
         kv += kv_recv[k].astype(jnp.float32)
-    sums = jnp.sum(kv[:, 2 * HD :], axis=1, keepdims=True) * (2.0 / HD)
+    sq = sq_part[:1, :]
+    for k in range(n_t - 1):
+        sq += sq_recv[k, :1, :]
+    row_at = lax.broadcasted_iota(jnp.int32, (rows + HALO, length), 0) + (t * rows - HALO)
+    sums = pick(lax.broadcasted_iota(jnp.int32, (rows + HALO, length), 1) == row_at, sq, 1)
     inverse = lax.rsqrt(sums / (feat * n_t) + epsilon)
     kv_bf = (kv[:, : 2 * HD] * inverse).astype(jnp.bfloat16)
     values = kv_bf[:, HD:]
@@ -435,22 +435,26 @@
     own_o.wait()
     for copy in o_last:
         copy.wait_recv()
-    for copy in gathers:
-        copy.wait_recv()
-
-    def out_tile(i, carry):
-        at = pl.ds(aligned(i, tile), tile)
-        total = packed[:, at].astype(jnp.float32)
-        for u in range(n_t):
+
+    for u in range(n_t):
+        for copy in gathers[u * (n_t - 1) : (u + 1) * (n_t - 1)]:
+            copy.wait_recv()
+
+        def out_tile(i, carry, u=u):
+            at = pl.ds(aligned(i, tile), tile)
+            total = packed[:, at].astype(jnp.float32) if u == 0 else acc[:, at]
             total += jnp.dot(
                 ctx[:, u * o_rows : (u + 1) * o_rows],
                 obuf[u, :, at],
                 preferred_element_type=jnp.float32,
             )
-        out[:, at] = jnp.where(valid_buf[:, :1] > 0.0, total, 0.0).astype(jnp.bfloat16)
-        return carry
-
-    lax.fori_loop(0, tiles, out_tile, 0)
+            if u < n_t - 1:
+                acc[:, at] = total
+            else:
+                out[:, at] = jnp.where(valid_buf[:, :1] > 0.0, total, 0.0).astype(jnp.bfloat16)
+            return carry
+
+        lax.fori_loop(0, tiles, out_tile, 0)
     for copy in started:
         copy.wait_send()
 
@@ -490,12 +494,15 @@
             pltpu.VMEM((length, feat), bf),
             pltpu.VMEM((length, feat), bf),
             pltpu.VMEM((length, n_t * qd), bf),
-            pltpu.VMEM((length + HALO, 3 * HD), bf),
+            pltpu.VMEM((length + HALO, 2 * HD), bf),
             pltpu.VMEM((n_t - 1, rows, n_t * qd), bf),
-            pltpu.VMEM((n_t - 1, rows + HALO, 3 * HD), bf),
+            pltpu.VMEM((n_t - 1, rows + HALO, 2 * HD), bf),
             pltpu.VMEM((length, n_t * qd), bf),
             pltpu.VMEM((length + HALO, HD), f32),
             pltpu.VMEM((length, HD), f32),
+            pltpu.VMEM((length, feat), f32),
+            pltpu.VMEM((8, length), f32),
+            pltpu.VMEM((n_t - 1, 8, length), f32),
             pltpu.SemaphoreType.DMA((copies,)),
             pltpu.SemaphoreType.DMA((copies,)),
             pltpu.SemaphoreType.DMA((8,)),

time: 62.7 us -> 62.3 us (level)
  no operation moved by 1% of the time
where the time goes in v3:
time: 62.3 us; the launch traced here: 62.2 us
  Pallas kernels  60.1 us (96%)
  local copies, waits for them, and re-layouts  2.06 us (3%)
    pallas_call x1, Pallas kernels, fused_body(): pl.pallas_call(functools.partial(fused_kernel, (n_dp, n_t, length, feat,...  60.1 us
    unnamed x1, local copies, waits for them, and re-layouts  2.06 us

profile of v3, /device:TPU:0, one launch (start us, length us, event | category | flops | bytes accessed | tf_op | source)
XLA Modules:
  0.0 62.2 jit_solution(7939949982552157475)
XLA Ops:
  0.0 60.1 %shard_map.82 = bf16[256,1536]{1,0:T(8,128)(2,1)} custom-call(s32[1,256]{1,0:T(1,128)} %bitcast.5, s32[8,32]{1,0:T(8,128)} %len_hbm.1, f32[1,6144]{1,0:T(1,128)} %bitcast.4, f32[16,128]{1,0:T(8,128)} %constant.2.clone.tab_hbm, bf16[256,1536]{1,0:T(8,128)(2,1)} %roll_hbm.1, bf16[6144,256]{1,0:T(8,128)(2,1)} %w_in.1, bf16[64,6144]{1,0:T(8,128)(2,1)} %bitcast.3, ...), custom_call_target="tpu_custom_call" | custom-call | tf_op jit(solution)/shard_map/pallas_call | solution.py:478
  60.1 2.1 %copy.10 = bf16[256,1536]{1,0:T(8,128)(2,1)} copy(bf16[256,1536]{1,0:T(8,128)(2,1)} %shard_map.82) | data formatting | bytes 1572864
